TPU v7x, 32 devices: a whole 2x2x4 slice. The times are simulated.
32 devices in a mesh: horiz: 8 (over y, x, core), lev: 4 (over z).
Axes of the slice: x: 2, y: 2, z: 4, core: 2. Of those that a mesh axis runs over, the one named last changes fastest.
Arguments:
- source_state: bfloat16 [5, 68, 32768], P(None, 'lev', 'horiz'), may hold values from -6 to 6
- intersection: int32 [40], P('horiz'), may hold values from 0 to 7, as said below
- index_map: int32 [40, 512], P('horiz'), may hold values from 0 to 4095
- blocks: bfloat16 [40, 512, 2048], P('horiz'), may hold values from -0.125 to 0.125
- bracket: int32 [127, 16384], P(None, ('horiz', 'lev')), may hold values from 0 to 66
- fraction: float32 [127, 16384], P(None, ('horiz', 'lev')), may hold values from 0 to 1
Outputs:
- target_state: bfloat16 [5, 127, 16384], P(None, None, ('horiz', 'lev'))
Inputs may be any that keep to these rules, and one draw needn't show every extreme that they name: For every target group g, intersection[g * 5] to intersection[g * 5 + 4] are the groups g - 2 to g + 2 modulo 8, each once, in some order.
All inputs are finite; a program needn't handle non-finite values.
Results may differ from a plain program's by a relative error of at most 0.0049.
Values may be sent and summed in bfloat16 or wider, within the bound.
A program may use at most 64 MiB of HBM per device.

v0:
```python
import functools

import jax
import jax.numpy as jnp
from jax import lax
from jax.experimental import pallas as pl
from jax.experimental.pallas import tpu as pltpu
from jax.sharding import PartitionSpec as P

MESH = pl.DeviceIdType.MESH
HIGH = 256


def round_up(value, step):
    return (value + step - 1) // step * step


def remap_kernel(
    groups, levs, depth,
    inter_hbm, index_hbm, source_hbm, blocks_hbm, out_ref,
    inter_ref, index_ref, tile, stack32, stack, weights, request, wanted, chosen, arrived, total, slab,
    inter_sem, index_sem, tile_sem, weight_sem, req_send, req_recv, val_send, val_recv, lev_send, lev_recv, own_sem,
):
    fields, slab_levels, cells = tile.shape
    rows = stack.shape[0]
    count = 2 * depth + 1
    me = lax.axis_index("horiz")
    my_lev = lax.axis_index("lev")
    columns = out_ref.shape[2]
    half = round_up(rows // 2, 16)
    cuts = [(0, half), (half, rows - half)]

    barrier = pltpu.get_barrier_semaphore()
    offsets = [o for o in range(-depth, depth + 1) if o != 0]
    for offset in offsets:
        pl.semaphore_signal(
            barrier, inc=1, device_id={"horiz": lax.rem(me + offset + groups, groups)}, device_id_type=MESH
        )
    for hop in range(1, levs):
        pl.semaphore_signal(
            barrier, inc=1, device_id={"lev": lax.rem(my_lev + hop, levs)}, device_id_type=MESH
        )

    inter_copy = pltpu.make_async_copy(inter_hbm, inter_ref, inter_sem)
    inter_copy.start()
    index_copy = pltpu.make_async_copy(index_hbm, index_ref, index_sem)
    index_copy.start()
    tile_copy = pltpu.make_async_copy(source_hbm, tile, tile_sem)
    tile_copy.start()
    inter_copy.wait()
    index_copy.wait()
    slots = []
    for place in range(count):
        group = lax.rem(me + place - depth + groups, groups)
        cells_wanted = jnp.zeros((1, index_ref.shape[1]), jnp.int32)
        slot = jnp.int32(0)
        for k in range(count):
            hit = (inter_ref[k] == group).astype(jnp.int32)
            cells_wanted = cells_wanted + index_ref[k : k + 1, :] * hit
            slot = jnp.where(inter_ref[k] == group, jnp.int32(k), slot)
        slots.append(slot)
        if place == depth:
            wanted[place] = cells_wanted
        else:
            request[place] = cells_wanted

    tile_copy.wait()
    weight_copies = []
    for part in range(levs):
        copy = pltpu.make_async_copy(
            blocks_hbm.at[:, :, pl.ds(part * columns, columns)], weights.at[:, part], weight_sem.at[part]
        )
        copy.start()
        weight_copies.append(copy)
    for field in range(fields):
        stack32[pl.ds(field * slab_levels, slab_levels), :] = tile[field].astype(jnp.float32)
    spare = rows - fields * slab_levels
    if spare:
        stack32[pl.ds(fields * slab_levels, spare), :] = jnp.zeros((spare, cells), jnp.float32)
    stack[...] = stack32[...].astype(jnp.bfloat16)

    pl.semaphore_wait(barrier, len(offsets) + levs - 1)

    def request_copy(place):
        return pltpu.make_async_remote_copy(
            src_ref=request.at[place],
            dst_ref=wanted.at[2 * depth - place],
            send_sem=req_send.at[place],
            recv_sem=req_recv.at[2 * depth - place],
            device_id={"horiz": lax.rem(me + place - depth + groups, groups)},
            device_id_type=MESH,
        )

    def value_copy(place, piece):
        first, size = cuts[piece]
        return pltpu.make_async_remote_copy(
            src_ref=chosen.at[place, pl.ds(first, size)],
            dst_ref=arrived.at[2 * depth - place, pl.ds(first, size)],
            send_sem=val_send.at[piece, place],
            recv_sem=val_recv.at[piece, 2 * depth - place],
            device_id={"horiz": lax.rem(me + place - depth + groups, groups)},
            device_id_type=MESH,
        )

    def lev_copy(hop, piece):
        block = pl.ds(*cuts[piece])
        if hop == 0:
            return pltpu.make_async_copy(slab.at[0, block], out_ref.at[my_lev, block], own_sem.at[piece])
        return pltpu.make_async_remote_copy(
            src_ref=slab.at[hop, block],
            dst_ref=out_ref.at[my_lev, block],
            send_sem=lev_send.at[piece, hop],
            recv_sem=lev_recv.at[piece, hop],
            device_id={"lev": lax.rem(my_lev + hop, levs)},
            device_id_type=MESH,
        )

    for reach in range(depth, 0, -1):
        request_copy(depth - reach).start()
        request_copy(depth + reach).start()

    ids = lax.broadcasted_iota(jnp.int32, (HIGH, 1), 0).astype(jnp.float32).astype(jnp.bfloat16)

    def select(place):
        cell = wanted[place]
        high = cell // HIGH
        low = (cell - high * HIGH).astype(jnp.float32)
        values = jnp.zeros((rows, cell.shape[1]), jnp.float32)
        for chunk in range(cells // HIGH):
            here = jnp.where(high == chunk, low, -1.0).astype(jnp.bfloat16)
            picker = jnp.where(ids == here, jnp.bfloat16(1), jnp.bfloat16(0))
            values += jnp.dot(
                stack[:, chunk * HIGH : (chunk + 1) * HIGH], picker, preferred_element_type=jnp.float32
            )
        return values.astype(jnp.bfloat16)

    arrived[depth] = select(depth)

    def serve(step, carry):
        reach = depth - step // 2
        place = depth + reach * (1 - 2 * (step % 2))
        request_copy(2 * depth - place).wait_recv()
        chosen[place] = select(place)
        value_copy(place, 0).start()
        return carry

    lax.fori_loop(0, 2 * depth, serve, 0)

    for reach in range(depth, 0, -1):
        value_copy(depth - reach, 1).start()
        value_copy(depth + reach, 1).start()
    for copy in weight_copies:
        copy.wait()
    order = [depth]
    for reach in range(depth, 0, -1):
        order += [depth - reach, depth + reach]
    for piece, (first, size) in enumerate(cuts):
        block = pl.ds(first, size)
        for number, place in enumerate(order):
            if number:
                value_copy(2 * depth - place, piece).wait_recv()
            values = arrived[place, block]
            for hop in list(range(1, levs)) + [0]:
                part = lax.rem(my_lev + hop, levs)
                term = jnp.dot(values, weights[slots[place], part], preferred_element_type=jnp.float32)
                if number == 0:
                    total[part, block] = term
                elif number < count - 1:
                    total[part, block] += term
                else:
                    slab[hop, block] = (total[part, block] + term).astype(jnp.bfloat16)
                    lev_copy(hop, piece).start()
    for piece in range(len(cuts)):
        for hop in range(levs):
            lev_copy(hop, piece).wait()
        for offset in offsets:
            value_copy(depth + offset, piece).wait_send()
    for offset in offsets:
        request_copy(depth + offset).wait_send()


def rows_at(table, index):
    numbers = lax.GatherDimensionNumbers(
        offset_dims=(),
        collapsed_slice_dims=(0,),
        start_index_map=(0,),
        operand_batching_dims=(1,),
        start_indices_batching_dims=(1,),
    )
    return lax.gather(
        table, index[..., None], numbers, slice_sizes=(1, 1), mode=lax.GatherScatterMode.PROMISE_IN_BOUNDS
    )


def levels_kernel(
    slab_levels, slabs_hbm, bracket_hbm, fraction_hbm, out_hbm,
    slabs_ref, brackets, fractions, raw, table, mixed_ref, slab_sem, bracket_sem, fraction_sem, out_sem,
):
    levs = slabs_hbm.shape[0]
    strips, fields, levels_out, lanes = mixed_ref.shape
    total = levs * slab_levels
    step = 16

    def strip_copy(strip):
        return pltpu.make_async_copy(
            mixed_ref.at[strip],
            out_hbm.at[:, :, pl.ds(pl.multiple_of(strip * lanes, lanes), lanes)],
            out_sem.at[strip],
        )

    def slab_copy(strip):
        return pltpu.make_async_copy(
            slabs_hbm.at[:, :, pl.ds(pl.multiple_of(strip * lanes, lanes), lanes)],
            slabs_ref.at[strip],
            slab_sem.at[strip],
        )

    def bracket_copy(strip):
        return pltpu.make_async_copy(
            bracket_hbm.at[:, pl.ds(pl.multiple_of(strip * lanes, lanes), lanes)],
            brackets.at[strip],
            bracket_sem.at[strip],
        )

    def fraction_copy(strip):
        return pltpu.make_async_copy(
            fraction_hbm.at[:, pl.ds(pl.multiple_of(strip * lanes, lanes), lanes)],
            fractions.at[strip],
            fraction_sem.at[strip],
        )

    for strip in range(strips):
        slab_copy(strip).start()
        bracket_copy(strip).start()
        fraction_copy(strip).start()

    def work(strip, carry):
        slab_copy(strip).wait()
        bracket_copy(strip).wait()
        fraction_copy(strip).wait()
        raw[...] = slabs_ref[strip].astype(jnp.float32)
        for field in range(fields):
            for lev in range(levs):
                table[field, pl.ds(lev * slab_levels, slab_levels), :] = raw[
                    lev, pl.ds(field * slab_levels, slab_levels), :
                ]
        for start in range(0, levels_out, step):
            size = min(step, levels_out - start)
            bracket = brackets[strip, start : start + size, :]
            upper = fractions[strip, start : start + size, :]
            if size < step:
                bracket = jnp.concatenate([bracket, jnp.zeros((step - size, lanes), jnp.int32)], axis=0)
                upper = jnp.concatenate([upper, jnp.zeros((step - size, lanes), jnp.float32)], axis=0)
            halves = [bracket[i : i + 8] for i in range(0, step, 8)]
            high = [half >> 3 for half in halves]
            low = [half & 7 for half in halves]
            below = [[jnp.zeros((8, lanes), jnp.float32) for _ in halves] for _ in range(fields)]
            above = [[jnp.zeros((8, lanes), jnp.float32) for _ in halves] for _ in range(fields)]
            for group in range((total - 2) // 8 + 1):
                masks = [h == group for h in high]
                for field in range(fields):
                    here = table[field, pl.ds(group * 8, 8), :]
                    over = table[field, pl.ds(group * 8 + 1, 8), :]
                    for i, mask in enumerate(masks):
                        below[field][i] = jnp.where(mask, rows_at(here, low[i]), below[field][i])
                        above[field][i] = jnp.where(mask, rows_at(over, low[i]), above[field][i])
            for field in range(fields):
                mixed = (1.0 - upper) * jnp.concatenate(below[field], axis=0) + upper * jnp.concatenate(
                    above[field], axis=0
                )
                mixed_ref[strip, field, start : start + size, :] = mixed[:size].astype(jnp.bfloat16)
        strip_copy(strip).start()
        return carry

    for field in range(fields):
        table[field, pl.ds(total, table.shape[1] - total), :] = jnp.zeros(
            (table.shape[1] - total, lanes), jnp.float32
        )
    lax.fori_loop(0, strips, work, 0)
    for strip in range(strips):
        strip_copy(strip).wait()


def local(levs, groups, source_state, intersection, index_map, blocks, bracket, fraction):
    fields, slab_levels, cells = source_state.shape
    count, wide, targets = blocks.shape
    depth = (count - 1) // 2
    rows = round_up(fields * slab_levels, 8)
    columns = targets // levs
    slabs = pl.pallas_call(
        functools.partial(remap_kernel, groups, levs, depth),
        name="remap",
        out_shape=jax.ShapeDtypeStruct((levs, rows, columns), jnp.bfloat16),
        in_specs=[
            pl.BlockSpec(memory_space=pltpu.HBM),
            pl.BlockSpec(memory_space=pltpu.HBM),
            pl.BlockSpec(memory_space=pltpu.HBM),
            pl.BlockSpec(memory_space=pltpu.HBM),
        ],
        out_specs=pl.BlockSpec(memory_space=pltpu.HBM),
        scratch_shapes=[
            pltpu.SMEM((count,), jnp.int32),
            pltpu.VMEM((count, wide), jnp.int32),
            pltpu.VMEM((fields, slab_levels, cells), jnp.bfloat16),
            pltpu.VMEM((rows, cells), jnp.float32),
            pltpu.VMEM((rows, cells), jnp.bfloat16),
            pltpu.VMEM((count, levs, wide, columns), jnp.bfloat16),
            pltpu.VMEM((count, 1, wide), jnp.int32),
            pltpu.VMEM((count, 1, wide), jnp.int32),
            pltpu.VMEM((count, rows, wide), jnp.bfloat16),
            pltpu.VMEM((count, rows, wide), jnp.bfloat16),
            pltpu.VMEM((levs, rows, columns), jnp.float32),
            pltpu.VMEM((levs, rows, columns), jnp.bfloat16),
            pltpu.SemaphoreType.DMA,
            pltpu.SemaphoreType.DMA,
            pltpu.SemaphoreType.DMA,
            pltpu.SemaphoreType.DMA((levs,)),
            pltpu.SemaphoreType.DMA((count,)),
            pltpu.SemaphoreType.DMA((count,)),
            pltpu.SemaphoreType.DMA((2, count)),
            pltpu.SemaphoreType.DMA((2, count)),
            pltpu.SemaphoreType.DMA((2, levs)),
            pltpu.SemaphoreType.DMA((2, levs)),
            pltpu.SemaphoreType.DMA((2,)),
        ],
        compiler_params=pltpu.CompilerParams(
            collective_id=0, has_side_effects=True, vmem_limit_bytes=67043328 - 1300 * 1024
        ),
        cost_estimate=pl.CostEstimate(
            flops=2 * rows * count * wide * (cells + targets),
            bytes_accessed=2 * blocks.size + 2 * source_state.size,
            transcendentals=0,
        ),
    )(intersection, index_map, source_state, blocks)
    levels_out, held = bracket.shape
    lanes = 128
    return pl.pallas_call(
        functools.partial(levels_kernel, slab_levels),
        name="levels",
        out_shape=jax.ShapeDtypeStruct((fields, levels_out, held), jnp.bfloat16),
        in_specs=[pl.BlockSpec(memory_space=pltpu.HBM)] * 3,
        out_specs=pl.BlockSpec(memory_space=pltpu.HBM),
        scratch_shapes=[
            pltpu.VMEM((held // lanes, levs, rows, lanes), jnp.bfloat16),
            pltpu.VMEM((held // lanes, levels_out, lanes), jnp.int32),
            pltpu.VMEM((held // lanes, levels_out, lanes), jnp.float32),
            pltpu.VMEM((levs, rows, lanes), jnp.float32),
            pltpu.VMEM((fields, round_up(levs * slab_levels, 8) + 8, lanes), jnp.float32),
            pltpu.VMEM((held // lanes, fields, levels_out, lanes), jnp.bfloat16),
            pltpu.SemaphoreType.DMA((held // lanes,)),
            pltpu.SemaphoreType.DMA((held // lanes,)),
            pltpu.SemaphoreType.DMA((held // lanes,)),
            pltpu.SemaphoreType.DMA((held // lanes,)),
        ],
        compiler_params=pltpu.CompilerParams(vmem_limit_bytes=67043328 - 700 * 1024),
    )(slabs, bracket, fraction)


def solution(mesh):
    in_specs = (
        P(None, "lev", "horiz"),
        P("horiz"),
        P("horiz", None),
        P("horiz", None, None),
        P(None, ("horiz", "lev")),
        P(None, ("horiz", "lev")),
    )
    out_specs = P(None, None, ("horiz", "lev"))
    body = functools.partial(local, mesh.shape["lev"], mesh.shape["horiz"])
    return jax.shard_map(body, mesh=mesh, in_specs=in_specs, out_specs=out_specs, check_vma=False)
```

profile of v0, /device:TPU:0, one launch (start us, length us, event | category | flops | bytes accessed | tf_op | source)
XLA Modules:
  0.0 28.9 jit_solution(12735060323866265517)
XLA Ops:
  0.0 25.1 %remap.1.slabs_hbm = bf16[4,88,512]{2,1,0:T(8,128)(2,1)} custom-call(s32[5]{0:T(128)} %inter_hbm.1, s32[5,512]{1,0:T(8,128)} %index_hbm.1, bf16[5,17,4096]{2,1,0:T(8,128)(2,1)} %source_hbm.1, bf16[5,512,2048]{2,1,0:T(8,128)(2,1)} %blocks_hbm.1), custom_call_target="tpu_custom_call" | custom-call | flops 2768240640 | bytes 11182080 | tf_op jit(solution)/shard_map/remap/pallas_call | solution.py:290
  25.1 3.8 %levels.1 = bf16[5,127,512]{2,1,0:T(8,128)(2,1)} custom-call(bf16[4,88,512]{2,1,0:T(8,128)(2,1)} %remap.1.slabs_hbm, s32[127,512]{1,0:T(8,128)} %bracket_hbm.1, f32[127,512]{1,0:T(8,128)} %fraction_hbm.1), custom_call_target="tpu_custom_call" | custom-call | tf_op jit(solution)/shard_map/levels/pallas_call | solution.py:337
where the time goes:
time: 29.1 us; the launch traced here: 28.9 us
  Pallas kernels  28.9 us (99%)
    pallas_call x1, Pallas kernels, local(): pl.pallas_call(functools.partial(remap_kernel, groups, levs, depth), name...  25.1 us
    pallas_call x1, Pallas kernels, local(): pl.pallas_call(functools.partial(levels_kernel, slab_levels), name='level...  3.8 us

commit v1 on v0

v1 whole, which is shorter than its diff:
```python
import functools

import jax
import jax.numpy as jnp
from jax import lax
from jax.experimental import pallas as pl
from jax.experimental.pallas import tpu as pltpu
from jax.sharding import PartitionSpec as P

MESH = pl.DeviceIdType.MESH
HIGH = 256
LANES = 128


def round_up(value, step):
    return (value + step - 1) // step * step


def row_plan(fields, slab_levels):
    whole = slab_levels // 16 * 16
    rest = slab_levels - whole
    extra = round_up(fields * rest, 8)
    base = round_up(extra, 16)
    return whole, rest, extra, base, base + fields * whole


def field_groups(fields):
    first = max(1, fields // 5)
    second = (fields - first + 1) // 2
    cuts = [0, first, first + second, fields]
    return [(a, b) for a, b in zip(cuts[:-1], cuts[1:]) if b > a]


def rows_at(table, index):
    numbers = lax.GatherDimensionNumbers(
        offset_dims=(),
        collapsed_slice_dims=(0,),
        start_index_map=(0,),
        operand_batching_dims=(1,),
        start_indices_batching_dims=(1,),
    )
    return lax.gather(
        table, index[..., None], numbers, slice_sizes=(1, 1), mode=lax.GatherScatterMode.PROMISE_IN_BOUNDS
    )


def regrid_kernel(
    groups, levs, depth,
    inter_hbm, index_hbm, source_hbm, blocks_hbm, bracket_hbm, fraction_hbm, out_ref,
    inter_ref, index_ref, tile, spare, stack, weights, request, wanted, chosen, arrived, total, slab, got,
    brackets, fractions, raw, table,
    inter_sem, index_sem, tile_sem, weight_sem, bracket_sem, fraction_sem,
    req_send, req_recv, val_send, val_recv, lev_send, lev_recv,
):
    fields, slab_levels, cells = tile.shape
    whole, rest, extra, base, rows = row_plan(fields, slab_levels)
    count = 2 * depth + 1
    wide = index_ref.shape[1]
    me = lax.axis_index("horiz")
    my_lev = lax.axis_index("lev")
    levels_out, columns = brackets.shape
    plan = field_groups(fields)
    chunks = [(base + a * whole, (b - a) * whole) for a, b in plan]
    parts = [[i] for i in range(len(chunks))]
    spans = list(chunks)
    if extra:
        parts[0].append(len(chunks))
        spans[0] = (0, base + chunks[0][1])
        chunks.append((0, extra))

    barrier = pltpu.get_barrier_semaphore()
    offsets = [o for o in range(-depth, depth + 1) if o != 0]
    for offset in offsets:
        pl.semaphore_signal(
            barrier, inc=1, device_id={"horiz": lax.rem(me + offset + groups, groups)}, device_id_type=MESH
        )
    for hop in range(1, levs):
        pl.semaphore_signal(
            barrier, inc=1, device_id={"lev": lax.rem(my_lev + hop, levs)}, device_id_type=MESH
        )

    inter_copy = pltpu.make_async_copy(inter_hbm, inter_ref, inter_sem)
    inter_copy.start()
    index_copy = pltpu.make_async_copy(index_hbm, index_ref, index_sem)
    index_copy.start()
    tile_copy = pltpu.make_async_copy(source_hbm, tile, tile_sem)
    tile_copy.start()
    inter_copy.wait()
    index_copy.wait()
    slots = []
    for place in range(count):
        group = lax.rem(me + place - depth + groups, groups)
        cells_wanted = jnp.zeros((1, wide), jnp.int32)
        slot = jnp.int32(0)
        for k in range(count):
            hit = (inter_ref[k] == group).astype(jnp.int32)
            cells_wanted = cells_wanted + index_ref[k : k + 1, :] * hit
            slot = jnp.where(inter_ref[k] == group, jnp.int32(k), slot)
        slots.append(slot)
        if place == depth:
            wanted[place] = cells_wanted
        else:
            request[place] = cells_wanted

    tile_copy.wait()
    weight_copies = []
    for part in range(levs):
        copy = pltpu.make_async_copy(
            blocks_hbm.at[:, :, pl.ds(part * columns, columns)], weights.at[:, part], weight_sem.at[part]
        )
        copy.start()
        weight_copies.append(copy)
    bracket_copy = pltpu.make_async_copy(bracket_hbm, brackets, bracket_sem)
    bracket_copy.start()
    fraction_copy = pltpu.make_async_copy(fraction_hbm, fractions, fraction_sem)
    fraction_copy.start()
    blocks_high = cells // HIGH
    if base:
        spare[...] = jnp.zeros(spare.shape, jnp.float32)
        for field in range(fields):
            if rest:
                spare[pl.ds(field * rest, rest), :] = tile[field, pl.ds(whole, rest), :].astype(jnp.float32)
    for chunk in range(blocks_high):
        lane = pl.ds(chunk * HIGH, HIGH)
        if base:
            stack[pl.ds(chunk * rows, base), :] = spare[:, lane].astype(jnp.bfloat16)
        for field in range(fields):
            stack[pl.ds(chunk * rows + base + field * whole, whole), :] = tile[field, pl.ds(0, whole), lane]

    def request_copy(place):
        return pltpu.make_async_remote_copy(
            src_ref=request.at[place],
            dst_ref=wanted.at[2 * depth - place],
            send_sem=req_send.at[place],
            recv_sem=req_recv.at[2 * depth - place],
            device_id={"horiz": lax.rem(me + place - depth + groups, groups)},
            device_id_type=MESH,
        )

    def value_copy(place, piece):
        first, size = chunks[piece]
        return pltpu.make_async_remote_copy(
            src_ref=chosen.at[place, pl.ds(first, size)],
            dst_ref=arrived.at[2 * depth - place, pl.ds(first, size)],
            send_sem=val_send.at[piece, place],
            recv_sem=val_recv.at[piece, 2 * depth - place],
            device_id={"horiz": lax.rem(me + place - depth + groups, groups)},
            device_id_type=MESH,
        )

    def lev_copy(hop, piece):
        block = pl.ds(*chunks[piece])
        return pltpu.make_async_remote_copy(
            src_ref=slab.at[hop, block],
            dst_ref=got.at[my_lev, block],
            send_sem=lev_send.at[piece, hop],
            recv_sem=lev_recv.at[piece, hop],
            device_id={"lev": lax.rem(my_lev + hop, levs)},
            device_id_type=MESH,
        )

    pl.semaphore_wait(barrier, len(offsets) + levs - 1)
    for reach in range(depth, 0, -1):
        request_copy(depth - reach).start()
        request_copy(depth + reach).start()

    ids = lax.broadcasted_iota(jnp.int32, (HIGH, 1), 0).astype(jnp.float32).astype(jnp.bfloat16)

    def select(place):
        cell = wanted[place]
        high = cell // HIGH
        low = (cell - high * HIGH).astype(jnp.float32).astype(jnp.bfloat16)
        picker = jnp.where(ids == low, jnp.bfloat16(1), jnp.bfloat16(0))
        found = jnp.dot(stack[...], picker, preferred_element_type=jnp.float32)
        values = jnp.zeros((rows, wide), jnp.float32)
        for chunk in range(blocks_high):
            values = jnp.where(high == chunk, found[chunk * rows : (chunk + 1) * rows], values)
        return values.astype(jnp.bfloat16)

    arrived[depth] = select(depth)

    lean = 1 - 2 * (me % 2)

    def order_place(step):
        reach = depth - step // 2
        return depth + reach * (2 * (step % 2) - 1) * lean

    def serve(step, carry):
        place = order_place(step)
        request_copy(2 * depth - place).wait_recv()
        chosen[place] = select(place)
        for piece in parts[0]:
            value_copy(place, piece).start()
        return carry

    last = 2 * depth - 1
    lax.fori_loop(0, last, serve, 0)
    for later in range(1, len(parts)):
        for step in range(last):
            for piece in parts[later]:
                value_copy(order_place(step), piece).start()
    near = order_place(last)
    request_copy(2 * depth - near).wait_recv()
    chosen[near] = select(near)
    for piece in range(len(chunks)):
        value_copy(near, piece).start()

    for copy in weight_copies:
        copy.wait()

    def slot_of(place):
        slot = slots[0]
        for k in range(1, count):
            slot = jnp.where(place == k, slots[k], slot)
        return slot

    values = arrived[depth]
    for part in range(levs):
        total[part] = jnp.dot(values, weights[slots[depth], part], preferred_element_type=jnp.float32)
    for piece in range(len(chunks)):
        value_copy(2 * depth - near, piece).wait_recv()
    values = arrived[near]
    near_slot = slot_of(near)
    for part in range(levs):
        total[part] += jnp.dot(values, weights[near_slot, part], preferred_element_type=jnp.float32)

    for number in range(len(parts)):
        block = pl.ds(*spans[number])
        for step in range(last):
            place = order_place(step)
            slot = slot_of(place)
            for piece in parts[number]:
                value_copy(2 * depth - place, piece).wait_recv()
            values = arrived[place, block]
            for hop in list(range(1, levs)) + [0]:
                part = lax.rem(my_lev + hop, levs)
                term = jnp.dot(values, weights[slot, part], preferred_element_type=jnp.float32)
                if step < last - 1:
                    total[part, block] += term
                elif hop:
                    slab[hop, block] = (total[part, block] + term).astype(jnp.bfloat16)
                    for piece in parts[number]:
                        lev_copy(hop, piece).start()
                else:
                    got[my_lev, block] = (total[part, block] + term).astype(jnp.bfloat16)

    bracket_copy.wait()
    fraction_copy.wait()
    levels_in = levs * slab_levels
    step_rows = 16
    table[:, pl.ds(levels_in, table.shape[1] - levels_in), :] = jnp.zeros(
        (table.shape[0], table.shape[1] - levels_in, LANES), jnp.float32
    )

    def interpolate(first, end):
        held = list(range(first, end))

        def work(strip, carry):
            lane = pl.ds(pl.multiple_of(strip * LANES, LANES), LANES)
            for lev in range(levs):
                if rest:
                    raw[lev] = got[lev, pl.ds(0, base), lane].astype(jnp.float32)
                for place, field in enumerate(held):
                    table[place, pl.ds(lev * slab_levels, whole), :] = got[
                        lev, pl.ds(base + field * whole, whole), lane
                    ].astype(jnp.float32)
                    if rest:
                        table[place, pl.ds(lev * slab_levels + whole, rest), :] = raw[
                            lev, pl.ds(field * rest, rest), :
                        ]
            for start in range(0, levels_out, step_rows):
                size = min(step_rows, levels_out - start)
                bracket = brackets[start : start + size, lane]
                upper = fractions[start : start + size, lane]
                if size < step_rows:
                    bracket = jnp.concatenate([bracket, jnp.zeros((step_rows - size, LANES), jnp.int32)], axis=0)
                    upper = jnp.concatenate([upper, jnp.zeros((step_rows - size, LANES), jnp.float32)], axis=0)
                halves = [bracket[i : i + 8] for i in range(0, step_rows, 8)]
                high = [half >> 3 for half in halves]
                low = [half & 7 for half in halves]
                below = [[jnp.zeros((8, LANES), jnp.float32) for _ in halves] for _ in held]
                above = [[jnp.zeros((8, LANES), jnp.float32) for _ in halves] for _ in held]
                for group in range((levels_in - 2) // 8 + 1):
                    masks = [h == group for h in high]
                    for place in range(len(held)):
                        here = table[place, pl.ds(group * 8, 8), :]
                        over = table[place, pl.ds(group * 8 + 1, 8), :]
                        for i, mask in enumerate(masks):
                            below[place][i] = jnp.where(mask, rows_at(here, low[i]), below[place][i])
                            above[place][i] = jnp.where(mask, rows_at(over, low[i]), above[place][i])
                for place, field in enumerate(held):
                    mixed = (1.0 - upper) * jnp.concatenate(below[place], axis=0) + upper * jnp.concatenate(
                        above[place], axis=0
                    )
                    out_ref[field, start : start + size, lane] = mixed[:size].astype(jnp.bfloat16)
            return carry

        lax.fori_loop(0, columns // LANES, work, 0)

    for number, (first, end) in enumerate(plan):
        for hop in range(1, levs):
            for piece in parts[number]:
                lev_copy(hop, piece).wait_recv()
        interpolate(first, end)

    for piece in range(len(chunks)):
        for hop in range(1, levs):
            lev_copy(hop, piece).wait_send()
        for offset in offsets:
            value_copy(depth + offset, piece).wait_send()
    for offset in offsets:
        request_copy(depth + offset).wait_send()


def store_kernel(held_ref, out_hbm, sem):
    copies = [
        pltpu.make_async_copy(held_ref.at[field], out_hbm.at[field], sem.at[field])
        for field in range(held_ref.shape[0])
    ]
    for copy in copies:
        copy.start()
    for copy in copies:
        copy.wait()


def local(levs, groups, source_state, intersection, index_map, blocks, bracket, fraction):
    fields, slab_levels, cells = source_state.shape
    count, wide, targets = blocks.shape
    depth = (count - 1) // 2
    whole, rest, extra, base, rows = row_plan(fields, slab_levels)
    columns = targets // levs
    levels_out = bracket.shape[0]
    plan = field_groups(fields)
    pieces = len(plan) + (1 if extra else 0)
    most = max(b - a for a, b in plan)
    bf16, f32, i32 = jnp.bfloat16, jnp.float32, jnp.int32
    dma = pltpu.SemaphoreType.DMA
    held = pl.pallas_call(
        functools.partial(regrid_kernel, groups, levs, depth),
        name="regrid",
        out_shape=pltpu.VMEM((fields, levels_out, columns), bf16),
        in_specs=[pl.BlockSpec(memory_space=pltpu.HBM)] * 6,
        out_specs=pl.BlockSpec(memory_space=pltpu.VMEM),
        scratch_shapes=[
            pltpu.SMEM((count,), i32),
            pltpu.VMEM((count, wide), i32),
            pltpu.VMEM((fields, slab_levels, cells), bf16),
            pltpu.VMEM((max(base, 8), cells), f32),
            pltpu.VMEM((cells // HIGH * rows, HIGH), bf16),
            pltpu.VMEM((count, levs, wide, columns), bf16),
            pltpu.VMEM((count, 1, wide), i32),
            pltpu.VMEM((count, 1, wide), i32),
            pltpu.VMEM((count, rows, wide), bf16),
            pltpu.VMEM((count, rows, wide), bf16),
            pltpu.VMEM((levs, rows, columns), f32),
            pltpu.VMEM((levs, rows, columns), bf16),
            pltpu.VMEM((levs, rows, columns), bf16),
            pltpu.VMEM((levels_out, columns), i32),
            pltpu.VMEM((levels_out, columns), f32),
            pltpu.VMEM((levs, max(base, 8), LANES), f32),
            pltpu.VMEM((most, round_up(levs * slab_levels, 8) + 8, LANES), f32),
            dma,
            dma,
            dma,
            dma((levs,)),
            dma,
            dma,
            dma((count,)),
            dma((count,)),
            dma((pieces, count)),
            dma((pieces, count)),
            dma((pieces, levs)),
            dma((pieces, levs)),
        ],
        compiler_params=pltpu.CompilerParams(
            collective_id=0, has_side_effects=True, vmem_limit_bytes=56 * 1024 * 1024
        ),
        cost_estimate=pl.CostEstimate(
            flops=2 * rows * count * wide * (cells + targets),
            bytes_accessed=2 * blocks.size + 2 * source_state.size,
            transcendentals=0,
        ),
    )(intersection, index_map, source_state, blocks, bracket, fraction)
    return pl.pallas_call(
        store_kernel,
        name="store",
        out_shape=jax.ShapeDtypeStruct(held.shape, bf16),
        in_specs=[pl.BlockSpec(memory_space=pltpu.VMEM)],
        out_specs=pl.BlockSpec(memory_space=pltpu.HBM),
        scratch_shapes=[dma((fields,))],
        compiler_params=pltpu.CompilerParams(vmem_limit_bytes=8 * 1024 * 1024),
    )(held)


def solution(mesh):
    in_specs = (
        P(None, "lev", "horiz"),
        P("horiz"),
        P("horiz", None),
        P("horiz", None, None),
        P(None, ("horiz", "lev")),
        P(None, ("horiz", "lev")),
    )
    out_specs = P(None, None, ("horiz", "lev"))
    body = functools.partial(local, mesh.shape["lev"], mesh.shape["horiz"])
    return jax.shard_map(body, mesh=mesh, in_specs=in_specs, out_specs=out_specs, check_vma=False)
```

time: 29.1 us -> 26.1 us (0.90)
  Pallas kernels: 28.9 us -> 25.9 us
    pallas_call x2, Pallas kernels: 28.9 us -> 25.9 us  [the longest x1 25 us: local(): pl.pallas_call(functools.partial(regrid_kernel, groups, levs, depth), nam...]
where the time goes in v1:
time: 26.1 us; the launch traced here: 25.9 us
  Pallas kernels  25.9 us (99%)
    pallas_call x1, Pallas kernels, local(): pl.pallas_call(functools.partial(regrid_kernel, groups, levs, depth), nam...  25 us
    pallas_call x1, Pallas kernels, local(): pl.pallas_call(store_kernel, name='store', out_shape=jax.ShapeDtypeStruct...  0.87 us

profile of v1, /device:TPU:0, one launch (start us, length us, event | category | flops | bytes accessed | tf_op | source)
XLA Modules:
  0.0 25.9 jit_solution(9571526375181858993)
XLA Ops:
  0.0 25.0 %regrid.1.held_ref = bf16[5,127,512]{2,1,0:T(8,128)(2,1)S(1)} custom-call(s32[5]{0:T(128)} %inter_hbm.1, s32[5,512]{1,0:T(8,128)} %index_hbm.1, bf16[5,17,4096]{2,1,0:T(8,128)(2,1)} %source_hbm.1, bf16[5,512,2048]{2,1,0:T(8,128)(2,1)} %blocks_hbm.1, s32[127,512]{1,0:T(8,128)} %bracket_hbm.1, f32[127,512]{1,0:T(8,128)} %fraction_hbm.1), custom_call_target="tpu_custom_call" | custom-call | flops 3019898880 | bytes 11182080 | tf_op jit(solution)/shard_map/regrid/pallas_call | solution.py:338
  25.0 0.9 %store.1 = bf16[5,127,512]{2,1,0:T(8,128)(2,1)} custom-call(bf16[5,127,512]{2,1,0:T(8,128)(2,1)S(1)} %regrid.1.held_ref), custom_call_target="tpu_custom_call" | custom-call | tf_op jit(solution)/shard_map/store/pallas_call | solution.py:384

commit v2 on v1

--- a/solution.py
+++ b/solution.py
@@ -47,7 +47,7 @@
 def regrid_kernel(
     groups, levs, depth,
     inter_hbm, index_hbm, source_hbm, blocks_hbm, bracket_hbm, fraction_hbm, out_ref,
-    inter_ref, index_ref, tile, spare, stack, weights, request, wanted, chosen, arrived, total, slab, got,
+    inter_ref, index_ref, tile, spare, first_rows, other_rows, weights, request, wanted, chosen, arrived, total, slab, got,
     brackets, fractions, raw, table,
     inter_sem, index_sem, tile_sem, weight_sem, bracket_sem, fraction_sem,
     req_send, req_recv, val_send, val_recv, lev_send, lev_recv,
@@ -85,6 +85,17 @@
     index_copy.start()
     tile_copy = pltpu.make_async_copy(source_hbm, tile, tile_sem)
     tile_copy.start()
+    weight_copies = []
+    for part in range(levs):
+        copy = pltpu.make_async_copy(
+            blocks_hbm.at[:, :, pl.ds(part * columns, columns)], weights.at[:, part], weight_sem.at[part]
+        )
+        copy.start()
+        weight_copies.append(copy)
+    bracket_copy = pltpu.make_async_copy(bracket_hbm, brackets, bracket_sem)
+    bracket_copy.start()
+    fraction_copy = pltpu.make_async_copy(fraction_hbm, fractions, fraction_sem)
+    fraction_copy.start()
     inter_copy.wait()
     index_copy.wait()
     slots = []
@@ -102,31 +113,6 @@
         else:
             request[place] = cells_wanted
 
-    tile_copy.wait()
-    weight_copies = []
-    for part in range(levs):
-        copy = pltpu.make_async_copy(
-            blocks_hbm.at[:, :, pl.ds(part * columns, columns)], weights.at[:, part], weight_sem.at[part]
-        )
-        copy.start()
-        weight_copies.append(copy)
-    bracket_copy = pltpu.make_async_copy(bracket_hbm, brackets, bracket_sem)
-    bracket_copy.start()
-    fraction_copy = pltpu.make_async_copy(fraction_hbm, fractions, fraction_sem)
-    fraction_copy.start()
-    blocks_high = cells // HIGH
-    if base:
-        spare[...] = jnp.zeros(spare.shape, jnp.float32)
-        for field in range(fields):
-            if rest:
-                spare[pl.ds(field * rest, rest), :] = tile[field, pl.ds(whole, rest), :].astype(jnp.float32)
-    for chunk in range(blocks_high):
-        lane = pl.ds(chunk * HIGH, HIGH)
-        if base:
-            stack[pl.ds(chunk * rows, base), :] = spare[:, lane].astype(jnp.bfloat16)
-        for field in range(fields):
-            stack[pl.ds(chunk * rows + base + field * whole, whole), :] = tile[field, pl.ds(0, whole), lane]
-
     def request_copy(place):
         return pltpu.make_async_remote_copy(
             src_ref=request.at[place],
@@ -148,14 +134,29 @@
             device_id_type=MESH,
         )
 
-    def lev_copy(hop, piece):
+    def dest_of(turn):
+        return turn + (turn >= my_lev).astype(jnp.int32)
+
+    def lev_copy(turn, piece):
         block = pl.ds(*chunks[piece])
         return pltpu.make_async_remote_copy(
-            src_ref=slab.at[hop, block],
+            src_ref=slab.at[turn, block],
             dst_ref=got.at[my_lev, block],
-            send_sem=lev_send.at[piece, hop],
-            recv_sem=lev_recv.at[piece, hop],
-            device_id={"lev": lax.rem(my_lev + hop, levs)},
+            send_sem=lev_send.at[piece, turn],
+            recv_sem=lev_recv.at[piece, my_lev],
+            device_id={"lev": dest_of(turn)},
+            device_id_type=MESH,
+        )
+
+    def lev_arrival(turn, piece):
+        block = pl.ds(*chunks[piece])
+        sender = dest_of(turn)
+        return pltpu.make_async_remote_copy(
+            src_ref=slab.at[turn, block],
+            dst_ref=got.at[sender, block],
+            send_sem=lev_send.at[piece, turn],
+            recv_sem=lev_recv.at[piece, sender],
+            device_id={"lev": sender},
             device_id_type=MESH,
         )
 
@@ -164,20 +165,43 @@
         request_copy(depth - reach).start()
         request_copy(depth + reach).start()
 
+    tile_copy.wait()
+    high_count = cells // HIGH
+    head = spans[0][1]
+    tail = rows - head
+    if base:
+        spare[...] = jnp.zeros(spare.shape, jnp.float32)
+        for field in range(fields):
+            if rest:
+                spare[pl.ds(field * rest, rest), :] = tile[field, pl.ds(whole, rest), :].astype(jnp.float32)
+    for chunk in range(high_count):
+        lane = pl.ds(chunk * HIGH, HIGH)
+        if base:
+            first_rows[pl.ds(chunk * head, base), :] = spare[:, lane].astype(jnp.bfloat16)
+        for field in range(fields):
+            if field < plan[0][1]:
+                spot = first_rows.at[pl.ds(chunk * head + base + field * whole, whole)]
+            else:
+                spot = other_rows.at[pl.ds(chunk * tail + base + field * whole - head, whole)]
+            spot[...] = tile[field, pl.ds(0, whole), lane]
+
     ids = lax.broadcasted_iota(jnp.int32, (HIGH, 1), 0).astype(jnp.float32).astype(jnp.bfloat16)
 
-    def select(place):
+    def select(place, held):
         cell = wanted[place]
         high = cell // HIGH
         low = (cell - high * HIGH).astype(jnp.float32).astype(jnp.bfloat16)
         picker = jnp.where(ids == low, jnp.bfloat16(1), jnp.bfloat16(0))
-        found = jnp.dot(stack[...], picker, preferred_element_type=jnp.float32)
-        values = jnp.zeros((rows, wide), jnp.float32)
-        for chunk in range(blocks_high):
-            values = jnp.where(high == chunk, found[chunk * rows : (chunk + 1) * rows], values)
+        found = jnp.dot(held[...], picker, preferred_element_type=jnp.float32)
+        size = held.shape[0] // high_count
+        values = jnp.zeros((size, wide), jnp.float32)
+        for chunk in range(high_count):
+            values = jnp.where(high == chunk, found[chunk * size : (chunk + 1) * size], values)
         return values.astype(jnp.bfloat16)
 
-    arrived[depth] = select(depth)
+    first_span, other_span = pl.ds(0, head), pl.ds(head, tail)
+    arrived[depth, first_span] = select(depth, first_rows)
+    arrived[depth, other_span] = select(depth, other_rows)
 
     lean = 1 - 2 * (me % 2)
 
@@ -185,23 +209,34 @@
         reach = depth - step // 2
         return depth + reach * (2 * (step % 2) - 1) * lean
 
+    last = 2 * depth - 1
+
     def serve(step, carry):
         place = order_place(step)
         request_copy(2 * depth - place).wait_recv()
-        chosen[place] = select(place)
+        chosen[place, first_span] = select(place, first_rows)
         for piece in parts[0]:
             value_copy(place, piece).start()
         return carry
 
-    last = 2 * depth - 1
     lax.fori_loop(0, last, serve, 0)
-    for later in range(1, len(parts)):
+
+    def serve_rest(step, carry):
+        place = order_place(step)
+        chosen[place, other_span] = select(place, other_rows)
+        for piece in parts[1]:
+            value_copy(place, piece).start()
+        return carry
+
+    lax.fori_loop(0, last, serve_rest, 0)
+    for later in range(2, len(parts)):
         for step in range(last):
             for piece in parts[later]:
                 value_copy(order_place(step), piece).start()
     near = order_place(last)
     request_copy(2 * depth - near).wait_recv()
-    chosen[near] = select(near)
+    chosen[near, first_span] = select(near, first_rows)
+    chosen[near, other_span] = select(near, other_rows)
     for piece in range(len(chunks)):
         value_copy(near, piece).start()
 
@@ -224,25 +259,36 @@
     for part in range(levs):
         total[part] += jnp.dot(values, weights[near_slot, part], preferred_element_type=jnp.float32)
 
+    def send_others(number):
+        for turn in range(1, levs - 1):
+            for piece in parts[number]:
+                lev_copy(turn, piece).start()
+
+    far = [order_place(step) for step in range(last)]
+    far_slots = [slot_of(place) for place in far]
     for number in range(len(parts)):
         block = pl.ds(*spans[number])
-        for step in range(last):
-            place = order_place(step)
-            slot = slot_of(place)
+        for place in far:
             for piece in parts[number]:
                 value_copy(2 * depth - place, piece).wait_recv()
-            values = arrived[place, block]
-            for hop in list(range(1, levs)) + [0]:
-                part = lax.rem(my_lev + hop, levs)
-                term = jnp.dot(values, weights[slot, part], preferred_element_type=jnp.float32)
-                if step < last - 1:
-                    total[part, block] += term
-                elif hop:
-                    slab[hop, block] = (total[part, block] + term).astype(jnp.bfloat16)
-                    for piece in parts[number]:
-                        lev_copy(hop, piece).start()
-                else:
-                    got[my_lev, block] = (total[part, block] + term).astype(jnp.bfloat16)
+        values = [arrived[place, block] for place in far]
+
+        def column_sum(part):
+            sums = total[part, block]
+            for value, slot in zip(values, far_slots):
+                sums += jnp.dot(value, weights[slot, part], preferred_element_type=jnp.float32)
+            return sums.astype(jnp.bfloat16)
+
+        slab[0, block] = column_sum(dest_of(0))
+        for piece in parts[number]:
+            lev_copy(0, piece).start()
+        if number == len(parts) - 1:
+            send_others(number - 1)
+        for turn in range(1, levs - 1):
+            slab[turn, block] = column_sum(dest_of(turn))
+        if number != len(parts) - 2:
+            send_others(number)
+        got[my_lev, block] = column_sum(my_lev)
 
     bracket_copy.wait()
     fraction_copy.wait()
@@ -298,14 +344,14 @@
         lax.fori_loop(0, columns // LANES, work, 0)
 
     for number, (first, end) in enumerate(plan):
-        for hop in range(1, levs):
+        for turn in range(levs - 1):
             for piece in parts[number]:
-                lev_copy(hop, piece).wait_recv()
+                lev_arrival(turn, piece).wait_recv()
         interpolate(first, end)
 
     for piece in range(len(chunks)):
-        for hop in range(1, levs):
-            lev_copy(hop, piece).wait_send()
+        for turn in range(levs - 1):
+            lev_copy(turn, piece).wait_send()
         for offset in offsets:
             value_copy(depth + offset, piece).wait_send()
     for offset in offsets:
@@ -333,6 +379,7 @@
     plan = field_groups(fields)
     pieces = len(plan) + (1 if extra else 0)
     most = max(b - a for a, b in plan)
+    head = base + plan[0][1] * whole
     bf16, f32, i32 = jnp.bfloat16, jnp.float32, jnp.int32
     dma = pltpu.SemaphoreType.DMA
     held = pl.pallas_call(
@@ -346,7 +393,8 @@
             pltpu.VMEM((count, wide), i32),
             pltpu.VMEM((fields, slab_levels, cells), bf16),
             pltpu.VMEM((max(base, 8), cells), f32),
-            pltpu.VMEM((cells // HIGH * rows, HIGH), bf16),
+            pltpu.VMEM((cells // HIGH * head, HIGH), bf16),
+            pltpu.VMEM((cells // HIGH * (rows - head), HIGH), bf16),
             pltpu.VMEM((count, levs, wide, columns), bf16),
             pltpu.VMEM((count, 1, wide), i32),
             pltpu.VMEM((count, 1, wide), i32),

time: 26.1 us -> 24.2 us (0.927)
  Pallas kernels: 25.9 us -> 24.1 us
    pallas_call x1, Pallas kernels: 25 us -> 23.2 us  [local(): pl.pallas_call(functools.partial(regrid_kernel, groups, levs, depth), nam...]
where the time goes in v2:
time: 24.2 us; the launch traced here: 24.1 us
  Pallas kernels  24.1 us (100%)
    pallas_call x1, Pallas kernels, local(): pl.pallas_call(functools.partial(regrid_kernel, groups, levs, depth), nam...  23.2 us
    pallas_call x1, Pallas kernels, local(): pl.pallas_call(store_kernel, name='store', out_shape=jax.ShapeDtypeStruct...  0.87 us

profile of v2, /device:TPU:0, one launch (start us, length us, event | category | flops | bytes accessed | tf_op | source)
XLA Modules:
  0.0 24.1 jit_solution(11023705371364445642)
XLA Ops:
  0.0 23.2 %regrid.1.held_ref = bf16[5,127,512]{2,1,0:T(8,128)(2,1)S(1)} custom-call(s32[5]{0:T(128)} %inter_hbm.1, s32[5,512]{1,0:T(8,128)} %index_hbm.1, bf16[5,17,4096]{2,1,0:T(8,128)(2,1)} %source_hbm.1, bf16[5,512,2048]{2,1,0:T(8,128)(2,1)} %blocks_hbm.1, s32[127,512]{1,0:T(8,128)} %bracket_hbm.1, f32[127,512]{1,0:T(8,128)} %fraction_hbm.1), custom_call_target="tpu_custom_call" | custom-call | flops 3019898880 | bytes 11182080 | tf_op jit(solution)/shard_map/regrid/pallas_call | solution.py:385
  23.2 0.9 %store.1 = bf16[5,127,512]{2,1,0:T(8,128)(2,1)} custom-call(bf16[5,127,512]{2,1,0:T(8,128)(2,1)S(1)} %regrid.1.held_ref), custom_call_target="tpu_custom_call" | custom-call | tf_op jit(solution)/shard_map/store/pallas_call | solution.py:432

commit v3 on v2

--- a/solution.py
+++ b/solution.py
@@ -27,7 +27,7 @@
 def field_groups(fields):
     first = max(1, fields // 5)
     second = (fields - first + 1) // 2
-    cuts = [0, first, first + second, fields]
+    cuts = [0, first, first + second, (first + second + fields) // 2, fields]
     return [(a, b) for a, b in zip(cuts[:-1], cuts[1:]) if b > a]
 
 
@@ -50,7 +50,7 @@
     inter_ref, index_ref, tile, spare, first_rows, other_rows, weights, request, wanted, chosen, arrived, total, slab, got,
     brackets, fractions, raw, table,
     inter_sem, index_sem, tile_sem, weight_sem, bracket_sem, fraction_sem,
-    req_send, req_recv, val_send, val_recv, lev_send, lev_recv,
+    req_send, req_recv, val_send, val_recv, lev_send, lev_recv, all_above,
 ):
     fields, slab_levels, cells = tile.shape
     whole, rest, extra, base, rows = row_plan(fields, slab_levels)
@@ -74,10 +74,14 @@
         pl.semaphore_signal(
             barrier, inc=1, device_id={"horiz": lax.rem(me + offset + groups, groups)}, device_id_type=MESH
         )
+    has_below, has_above = my_lev > 0, my_lev < levs - 1
+
+    def tell(semaphore, lev):
+        pl.semaphore_signal(semaphore, inc=1, device_id={"lev": lev}, device_id_type=MESH)
+
     for hop in range(1, levs):
-        pl.semaphore_signal(
-            barrier, inc=1, device_id={"lev": lax.rem(my_lev + hop, levs)}, device_id_type=MESH
-        )
+        pl.when(my_lev + hop < levs)(functools.partial(tell, barrier, my_lev + hop))
+    greeted = len(offsets) + my_lev
 
     inter_copy = pltpu.make_async_copy(inter_hbm, inter_ref, inter_sem)
     inter_copy.start()
@@ -85,13 +89,11 @@
     index_copy.start()
     tile_copy = pltpu.make_async_copy(source_hbm, tile, tile_sem)
     tile_copy.start()
-    weight_copies = []
     for part in range(levs):
         copy = pltpu.make_async_copy(
-            blocks_hbm.at[:, :, pl.ds(part * columns, columns)], weights.at[:, part], weight_sem.at[part]
+            blocks_hbm.at[:, :, pl.ds(part * columns, columns)], weights.at[:, part], weight_sem
         )
         copy.start()
-        weight_copies.append(copy)
     bracket_copy = pltpu.make_async_copy(bracket_hbm, brackets, bracket_sem)
     bracket_copy.start()
     fraction_copy = pltpu.make_async_copy(fraction_hbm, fractions, fraction_sem)
@@ -117,50 +119,54 @@
         return pltpu.make_async_remote_copy(
             src_ref=request.at[place],
             dst_ref=wanted.at[2 * depth - place],
-            send_sem=req_send.at[place],
+            send_sem=req_send,
             recv_sem=req_recv.at[2 * depth - place],
             device_id={"horiz": lax.rem(me + place - depth + groups, groups)},
             device_id_type=MESH,
         )
 
-    def value_copy(place, piece):
+    def value_copy(place, piece, sign):
         first, size = chunks[piece]
         return pltpu.make_async_remote_copy(
             src_ref=chosen.at[place, pl.ds(first, size)],
             dst_ref=arrived.at[2 * depth - place, pl.ds(first, size)],
-            send_sem=val_send.at[piece, place],
-            recv_sem=val_recv.at[piece, 2 * depth - place],
+            send_sem=val_send,
+            recv_sem=val_recv.at[sign],
             device_id={"horiz": lax.rem(me + place - depth + groups, groups)},
             device_id_type=MESH,
         )
 
+    def tally(ref, send_sem, recv_sem):
+        return pltpu.make_async_remote_copy(
+            src_ref=ref,
+            dst_ref=ref,
+            send_sem=send_sem,
+            recv_sem=recv_sem,
+            device_id={"lev": dest_of(0)},
+            device_id_type=MESH,
+        )
+
+    weight_of = [sum(chunks[piece][1] for piece in part) for part in parts]
+    sent_rows = sum(weight_of)
+
+    upper = 2 * my_lev >= levs
+
     def dest_of(turn):
         return turn + (turn >= my_lev).astype(jnp.int32)
 
-    def lev_copy(turn, piece):
+    def lev_copy(turn, number, piece):
         block = pl.ds(*chunks[piece])
         return pltpu.make_async_remote_copy(
             src_ref=slab.at[turn, block],
             dst_ref=got.at[my_lev, block],
-            send_sem=lev_send.at[piece, turn],
-            recv_sem=lev_recv.at[piece, my_lev],
+            send_sem=lev_send,
+            recv_sem=lev_recv.at[number],
             device_id={"lev": dest_of(turn)},
             device_id_type=MESH,
         )
 
-    def lev_arrival(turn, piece):
-        block = pl.ds(*chunks[piece])
-        sender = dest_of(turn)
-        return pltpu.make_async_remote_copy(
-            src_ref=slab.at[turn, block],
-            dst_ref=got.at[sender, block],
-            send_sem=lev_send.at[piece, turn],
-            recv_sem=lev_recv.at[piece, sender],
-            device_id={"lev": sender},
-            device_id_type=MESH,
-        )
-
-    pl.semaphore_wait(barrier, len(offsets) + levs - 1)
+    pl.semaphore_wait(barrier, greeted)
+    pl.when((my_lev == levs - 1) & has_below)(lambda: tell(all_above, my_lev - 1))
     for reach in range(depth, 0, -1):
         request_copy(depth - reach).start()
         request_copy(depth + reach).start()
@@ -203,6 +209,13 @@
     arrived[depth, first_span] = select(depth, first_rows)
     arrived[depth, other_span] = select(depth, other_rows)
 
+    def hand_down():
+        pl.semaphore_wait(all_above, 1)
+        tell(all_above, my_lev - 1)
+
+    between = has_below & has_above
+    pl.when(between & upper)(hand_down)
+
     lean = 1 - 2 * (me % 2)
 
     def order_place(step):
@@ -216,32 +229,33 @@
         request_copy(2 * depth - place).wait_recv()
         chosen[place, first_span] = select(place, first_rows)
         for piece in parts[0]:
-            value_copy(place, piece).start()
+            value_copy(place, piece, 0).start()
         return carry
 
     lax.fori_loop(0, last, serve, 0)
+
+    pl.when(between & jnp.logical_not(upper))(hand_down)
 
     def serve_rest(step, carry):
         place = order_place(step)
         chosen[place, other_span] = select(place, other_rows)
         for piece in parts[1]:
-            value_copy(place, piece).start()
+            value_copy(place, piece, 1).start()
         return carry
 
     lax.fori_loop(0, last, serve_rest, 0)
     for later in range(2, len(parts)):
         for step in range(last):
             for piece in parts[later]:
-                value_copy(order_place(step), piece).start()
+                value_copy(order_place(step), piece, later).start()
     near = order_place(last)
     request_copy(2 * depth - near).wait_recv()
     chosen[near, first_span] = select(near, first_rows)
     chosen[near, other_span] = select(near, other_rows)
     for piece in range(len(chunks)):
-        value_copy(near, piece).start()
-
-    for copy in weight_copies:
-        copy.wait()
+        value_copy(near, piece, len(parts)).start()
+
+    pltpu.make_async_copy(weights, weights, weight_sem).wait()
 
     def slot_of(place):
         slot = slots[0]
@@ -252,8 +266,7 @@
     values = arrived[depth]
     for part in range(levs):
         total[part] = jnp.dot(values, weights[slots[depth], part], preferred_element_type=jnp.float32)
-    for piece in range(len(chunks)):
-        value_copy(2 * depth - near, piece).wait_recv()
+    tally(arrived.at[0, pl.ds(0, sent_rows)], val_send, val_recv.at[len(parts)]).wait_recv()
     values = arrived[near]
     near_slot = slot_of(near)
     for part in range(levs):
@@ -262,33 +275,42 @@
     def send_others(number):
         for turn in range(1, levs - 1):
             for piece in parts[number]:
-                lev_copy(turn, piece).start()
-
+                lev_copy(turn, number, piece).start()
+
+    if levs > 1:
+        pl.when(my_lev == 0)(lambda: pl.semaphore_wait(all_above, 1))
     far = [order_place(step) for step in range(last)]
     far_slots = [slot_of(place) for place in far]
     for number in range(len(parts)):
-        block = pl.ds(*spans[number])
-        for place in far:
-            for piece in parts[number]:
-                value_copy(2 * depth - place, piece).wait_recv()
-        values = [arrived[place, block] for place in far]
-
-        def column_sum(part):
+        tally(arrived.at[pl.ds(0, last), pl.ds(0, weight_of[number])], val_send, val_recv.at[number]).wait_recv()
+
+        def column_sum(part, block, values):
             sums = total[part, block]
             for value, slot in zip(values, far_slots):
                 sums += jnp.dot(value, weights[slot, part], preferred_element_type=jnp.float32)
             return sums.astype(jnp.bfloat16)
 
-        slab[0, block] = column_sum(dest_of(0))
+        block = pl.ds(*spans[number])
+        values = [arrived[place, block] for place in far]
+        slab[0, block] = column_sum(dest_of(0), block, values)
         for piece in parts[number]:
-            lev_copy(0, piece).start()
+            lev_copy(0, number, piece).start()
+        if number == len(parts) - 2:
+            continue
+        members = [number]
         if number == len(parts) - 1:
-            send_others(number - 1)
+            pl.when(upper)(functools.partial(send_others, len(parts) - 3))
+            members = [number - 1, number]
+            block = pl.ds(spans[number - 1][0], spans[number - 1][1] + spans[number][1])
+            values = [arrived[place, block] for place in far]
         for turn in range(1, levs - 1):
-            slab[turn, block] = column_sum(dest_of(turn))
-        if number != len(parts) - 2:
-            send_others(number)
-        got[my_lev, block] = column_sum(my_lev)
+            slab[turn, block] = column_sum(dest_of(turn), block, values)
+        got[my_lev, block] = column_sum(my_lev, block, values)
+        for member in members:
+            if member != len(parts) - 3:
+                send_others(member)
+            else:
+                pl.when(jnp.logical_not(upper))(functools.partial(send_others, member))
 
     bracket_copy.wait()
     fraction_copy.wait()
@@ -344,24 +366,17 @@
         lax.fori_loop(0, columns // LANES, work, 0)
 
     for number, (first, end) in enumerate(plan):
-        for turn in range(levs - 1):
-            for piece in parts[number]:
-                lev_arrival(turn, piece).wait_recv()
+        tally(got.at[pl.ds(0, levs - 1), pl.ds(0, weight_of[number])], lev_send, lev_recv.at[number]).wait_recv()
         interpolate(first, end)
 
-    for piece in range(len(chunks)):
-        for turn in range(levs - 1):
-            lev_copy(turn, piece).wait_send()
-        for offset in offsets:
-            value_copy(depth + offset, piece).wait_send()
-    for offset in offsets:
-        request_copy(depth + offset).wait_send()
+    tally(slab.at[:, pl.ds(0, sent_rows)], lev_send, lev_recv.at[0]).wait_send()
+    tally(chosen.at[pl.ds(0, 2 * depth), pl.ds(0, sent_rows)], val_send, val_recv.at[0]).wait_send()
+    tally(request.at[pl.ds(0, 2 * depth)], req_send, req_recv.at[0]).wait_send()
 
 
 def store_kernel(held_ref, out_hbm, sem):
     copies = [
-        pltpu.make_async_copy(held_ref.at[field], out_hbm.at[field], sem.at[field])
-        for field in range(held_ref.shape[0])
+        pltpu.make_async_copy(held_ref, out_hbm, sem)
     ]
     for copy in copies:
         copy.start()
@@ -377,7 +392,6 @@
     columns = targets // levs
     levels_out = bracket.shape[0]
     plan = field_groups(fields)
-    pieces = len(plan) + (1 if extra else 0)
     most = max(b - a for a, b in plan)
     head = base + plan[0][1] * whole
     bf16, f32, i32 = jnp.bfloat16, jnp.float32, jnp.int32
@@ -401,7 +415,7 @@
             pltpu.VMEM((count, rows, wide), bf16),
             pltpu.VMEM((count, rows, wide), bf16),
             pltpu.VMEM((levs, rows, columns), f32),
-            pltpu.VMEM((levs, rows, columns), bf16),
+            pltpu.VMEM((levs - 1, rows, columns), bf16),
             pltpu.VMEM((levs, rows, columns), bf16),
             pltpu.VMEM((levels_out, columns), i32),
             pltpu.VMEM((levels_out, columns), f32),
@@ -410,15 +424,16 @@
             dma,
             dma,
             dma,
-            dma((levs,)),
+            dma,
+            dma,
             dma,
             dma,
             dma((count,)),
-            dma((count,)),
-            dma((pieces, count)),
-            dma((pieces, count)),
-            dma((pieces, levs)),
-            dma((pieces, levs)),
+            dma,
+            dma((len(plan) + 1,)),
+            dma,
+            dma((len(plan),)),
+            pltpu.SemaphoreType.REGULAR,
         ],
         compiler_params=pltpu.CompilerParams(
             collective_id=0, has_side_effects=True, vmem_limit_bytes=56 * 1024 * 1024
@@ -435,7 +450,7 @@
         out_shape=jax.ShapeDtypeStruct(held.shape, bf16),
         in_specs=[pl.BlockSpec(memory_space=pltpu.VMEM)],
         out_specs=pl.BlockSpec(memory_space=pltpu.HBM),
-        scratch_shapes=[dma((fields,))],
+        scratch_shapes=[dma],
         compiler_params=pltpu.CompilerParams(vmem_limit_bytes=8 * 1024 * 1024),
     )(held)
 

time: 24.2 us -> 22.9 us (0.946)
  the two profiles are of different devices: /device:TPU:0 before, /device:TPU:11 now
where the time goes in v3:
time: 22.9 us; the launch traced here: 22.7 us
  Pallas kernels  22.7 us (99%)
    pallas_call x1, Pallas kernels, local(): pl.pallas_call(functools.partial(regrid_kernel, groups, levs, depth), nam...  21.9 us
    pallas_call x1, Pallas kernels, local(): pl.pallas_call(store_kernel, name='store', out_shape=jax.ShapeDtypeStruct...  0.85 us

profile of v3, /device:TPU:11, one launch (start us, length us, event | category | flops | bytes accessed | tf_op | source)
XLA Modules:
  0.0 22.7 jit_solution(4565446752349751011)
XLA Ops:
  0.0 21.9 %regrid.1.held_ref = bf16[5,127,512]{2,1,0:T(8,128)(2,1)S(1)} custom-call(s32[5]{0:T(128)} %inter_hbm.1, s32[5,512]{1,0:T(8,128)} %index_hbm.1, bf16[5,17,4096]{2,1,0:T(8,128)(2,1)} %source_hbm.1, bf16[5,512,2048]{2,1,0:T(8,128)(2,1)} %blocks_hbm.1, s32[127,512]{1,0:T(8,128)} %bracket_hbm.1, f32[127,512]{1,0:T(8,128)} %fraction_hbm.1), custom_call_target="tpu_custom_call" | custom-call | flops 3019898880 | bytes 11182080 | tf_op jit(solution)/shard_map/regrid/pallas_call | solution.py:399
  21.9 0.8 %store.1 = bf16[5,127,512]{2,1,0:T(8,128)(2,1)} custom-call(bf16[5,127,512]{2,1,0:T(8,128)(2,1)S(1)} %regrid.1.held_ref), custom_call_target="tpu_custom_call" | custom-call | tf_op jit(solution)/shard_map/store/pallas_call | solution.py:447

commit v4 on v3

--- a/solution.py
+++ b/solution.py
@@ -154,11 +154,21 @@
     def dest_of(turn):
         return turn + (turn >= my_lev).astype(jnp.int32)
 
-    def lev_copy(turn, number, piece):
+    sides = [(0, columns // 2), (columns // 2, columns // 2)]
+
+    def lev_copies(turn, number):
+        spread = sides if number == len(parts) - 1 else [(0, columns)]
+        return [
+            lev_copy(turn, number + side, piece, pl.ds(*lane))
+            for side, lane in enumerate(spread)
+            for piece in parts[number]
+        ]
+
+    def lev_copy(turn, number, piece, lane):
         block = pl.ds(*chunks[piece])
         return pltpu.make_async_remote_copy(
-            src_ref=slab.at[turn, block],
-            dst_ref=got.at[my_lev, block],
+            src_ref=slab.at[turn, block, lane],
+            dst_ref=got.at[my_lev, block, lane],
             send_sem=lev_send,
             recv_sem=lev_recv.at[number],
             device_id={"lev": dest_of(turn)},
@@ -224,6 +234,13 @@
 
     last = 2 * depth - 1
 
+    near = order_place(last)
+    request_copy(2 * depth - near).wait_recv()
+    chosen[near, first_span] = select(near, first_rows)
+    chosen[near, other_span] = select(near, other_rows)
+    for piece in range(len(chunks)):
+        value_copy(near, piece, len(parts)).start()
+
     def serve(step, carry):
         place = order_place(step)
         request_copy(2 * depth - place).wait_recv()
@@ -248,13 +265,6 @@
         for step in range(last):
             for piece in parts[later]:
                 value_copy(order_place(step), piece, later).start()
-    near = order_place(last)
-    request_copy(2 * depth - near).wait_recv()
-    chosen[near, first_span] = select(near, first_rows)
-    chosen[near, other_span] = select(near, other_rows)
-    for piece in range(len(chunks)):
-        value_copy(near, piece, len(parts)).start()
-
     pltpu.make_async_copy(weights, weights, weight_sem).wait()
 
     def slot_of(place):
@@ -263,19 +273,17 @@
             slot = jnp.where(place == k, slots[k], slot)
         return slot
 
-    values = arrived[depth]
+    tally(arrived.at[0, pl.ds(0, sent_rows)], val_send, val_recv.at[len(parts)]).wait_recv()
+    beside = [(arrived[depth], slots[depth]), (arrived[near], slot_of(near))]
     for part in range(levs):
-        total[part] = jnp.dot(values, weights[slots[depth], part], preferred_element_type=jnp.float32)
-    tally(arrived.at[0, pl.ds(0, sent_rows)], val_send, val_recv.at[len(parts)]).wait_recv()
-    values = arrived[near]
-    near_slot = slot_of(near)
-    for part in range(levs):
-        total[part] += jnp.dot(values, weights[near_slot, part], preferred_element_type=jnp.float32)
+        total[part] = sum(
+            jnp.dot(value, weights[slot, part], preferred_element_type=jnp.float32) for value, slot in beside
+        )
 
     def send_others(number):
         for turn in range(1, levs - 1):
-            for piece in parts[number]:
-                lev_copy(turn, number, piece).start()
+            for copy in lev_copies(turn, number):
+                copy.start()
 
     if levs > 1:
         pl.when(my_lev == 0)(lambda: pl.semaphore_wait(all_above, 1))
@@ -284,17 +292,24 @@
     for number in range(len(parts)):
         tally(arrived.at[pl.ds(0, last), pl.ds(0, weight_of[number])], val_send, val_recv.at[number]).wait_recv()
 
-        def column_sum(part, block, values):
-            sums = total[part, block]
+        def column_sum(part, block, values, lane=pl.ds(0, columns)):
+            sums = total[part, block, lane]
             for value, slot in zip(values, far_slots):
-                sums += jnp.dot(value, weights[slot, part], preferred_element_type=jnp.float32)
+                sums += jnp.dot(value, weights[slot, part, :, lane], preferred_element_type=jnp.float32)
             return sums.astype(jnp.bfloat16)
 
         block = pl.ds(*spans[number])
         values = [arrived[place, block] for place in far]
-        slab[0, block] = column_sum(dest_of(0), block, values)
-        for piece in parts[number]:
-            lev_copy(0, number, piece).start()
+        copies = lev_copies(0, number)
+        if number == len(parts) - 1:
+            for side, copy in zip(sides, copies):
+                lane = pl.ds(*side)
+                slab[0, block, lane] = column_sum(dest_of(0), block, values, lane)
+                copy.start()
+        else:
+            slab[0, block] = column_sum(dest_of(0), block, values)
+            for copy in copies:
+                copy.start()
         if number == len(parts) - 2:
             continue
         members = [number]
@@ -320,7 +335,7 @@
         (table.shape[0], table.shape[1] - levels_in, LANES), jnp.float32
     )
 
-    def interpolate(first, end):
+    def interpolate(first, end, low_strip, high_strip):
         held = list(range(first, end))
 
         def work(strip, carry):
@@ -346,16 +361,28 @@
                 halves = [bracket[i : i + 8] for i in range(0, step_rows, 8)]
                 high = [half >> 3 for half in halves]
                 low = [half & 7 for half in halves]
-                below = [[jnp.zeros((8, LANES), jnp.float32) for _ in halves] for _ in held]
-                above = [[jnp.zeros((8, LANES), jnp.float32) for _ in halves] for _ in held]
-                for group in range((levels_in - 2) // 8 + 1):
-                    masks = [h == group for h in high]
-                    for place in range(len(held)):
-                        here = table[place, pl.ds(group * 8, 8), :]
-                        over = table[place, pl.ds(group * 8 + 1, 8), :]
-                        for i, mask in enumerate(masks):
-                            below[place][i] = jnp.where(mask, rows_at(here, low[i]), below[place][i])
-                            above[place][i] = jnp.where(mask, rows_at(over, low[i]), above[place][i])
+                counts = (levels_in - 2) // 8 + 1
+                bits = max(1, (counts - 1).bit_length())
+                turns = [[(h & (1 << bit)) != 0 for bit in range(bits)] for h in high]
+
+                def choose(place, first, size, i):
+                    if size == 1:
+                        here = table[place, pl.ds(first * 8, 8), :]
+                        over = table[place, pl.ds(first * 8 + 1, 8), :]
+                        return rows_at(here, low[i]), rows_at(over, low[i])
+                    half = size // 2
+                    left = choose(place, first, half, i)
+                    if first + half >= counts:
+                        return left
+                    right = choose(place, first + half, half, i)
+                    mask = turns[i][half.bit_length() - 1]
+                    return tuple(jnp.where(mask, b, a) for a, b in zip(left, right))
+
+                below = [[None] * len(halves) for _ in held]
+                above = [[None] * len(halves) for _ in held]
+                for place in range(len(held)):
+                    for i in range(len(halves)):
+                        below[place][i], above[place][i] = choose(place, 0, 1 << bits, i)
                 for place, field in enumerate(held):
                     mixed = (1.0 - upper) * jnp.concatenate(below[place], axis=0) + upper * jnp.concatenate(
                         above[place], axis=0
@@ -363,11 +390,13 @@
                     out_ref[field, start : start + size, lane] = mixed[:size].astype(jnp.bfloat16)
             return carry
 
-        lax.fori_loop(0, columns // LANES, work, 0)
+        lax.fori_loop(low_strip, high_strip, work, 0)
 
     for number, (first, end) in enumerate(plan):
-        tally(got.at[pl.ds(0, levs - 1), pl.ds(0, weight_of[number])], lev_send, lev_recv.at[number]).wait_recv()
-        interpolate(first, end)
+        for side, (left, width) in enumerate(sides if number == len(parts) - 1 else [(0, columns)]):
+            landed = got.at[pl.ds(0, levs - 1), pl.ds(0, weight_of[number]), pl.ds(0, width)]
+            tally(landed, lev_send, lev_recv.at[number + side]).wait_recv()
+            interpolate(first, end, left // LANES, (left + width) // LANES)
 
     tally(slab.at[:, pl.ds(0, sent_rows)], lev_send, lev_recv.at[0]).wait_send()
     tally(chosen.at[pl.ds(0, 2 * depth), pl.ds(0, sent_rows)], val_send, val_recv.at[0]).wait_send()
@@ -432,7 +461,7 @@
             dma,
             dma((len(plan) + 1,)),
             dma,
-            dma((len(plan),)),
+            dma((len(plan) + 1,)),
             pltpu.SemaphoreType.REGULAR,
         ],
         compiler_params=pltpu.CompilerParams(

time: 22.9 us -> 22.7 us (level)
  no operation moved by 1% of the time
where the time goes in v4:
time: 22.7 us; the launch traced here: 22.6 us
  Pallas kernels  22.6 us (100%)
    pallas_call x1, Pallas kernels, local(): pl.pallas_call(functools.partial(regrid_kernel, groups, levs, depth), nam...  21.7 us
    pallas_call x1, Pallas kernels, local(): pl.pallas_call(store_kernel, name='store', out_shape=jax.ShapeDtypeStruct...  0.85 us

profile of v4, /device:TPU:11, one launch (start us, length us, event | category | flops | bytes accessed | tf_op | source)
XLA Modules:
  0.0 22.6 jit_solution(12116949317212007832)
XLA Ops:
  0.0 21.7 %regrid.1.held_ref = bf16[5,127,512]{2,1,0:T(8,128)(2,1)S(1)} custom-call(s32[5]{0:T(128)} %inter_hbm.1, s32[5,512]{1,0:T(8,128)} %index_hbm.1, bf16[5,17,4096]{2,1,0:T(8,128)(2,1)} %source_hbm.1, bf16[5,512,2048]{2,1,0:T(8,128)(2,1)} %blocks_hbm.1, s32[127,512]{1,0:T(8,128)} %bracket_hbm.1, f32[127,512]{1,0:T(8,128)} %fraction_hbm.1), custom_call_target="tpu_custom_call" | custom-call | flops 3019898880 | bytes 11182080 | tf_op jit(solution)/shard_map/regrid/pallas_call | solution.py:428
  21.7 0.8 %store.1 = bf16[5,127,512]{2,1,0:T(8,128)(2,1)} custom-call(bf16[5,127,512]{2,1,0:T(8,128)(2,1)S(1)} %regrid.1.held_ref), custom_call_target="tpu_custom_call" | custom-call | tf_op jit(solution)/shard_map/store/pallas_call | solution.py:476

commit v5 on v4

--- a/solution.py
+++ b/solution.py
@@ -234,13 +234,6 @@
 
     last = 2 * depth - 1
 
-    near = order_place(last)
-    request_copy(2 * depth - near).wait_recv()
-    chosen[near, first_span] = select(near, first_rows)
-    chosen[near, other_span] = select(near, other_rows)
-    for piece in range(len(chunks)):
-        value_copy(near, piece, len(parts)).start()
-
     def serve(step, carry):
         place = order_place(step)
         request_copy(2 * depth - place).wait_recv()
@@ -250,6 +243,11 @@
         return carry
 
     lax.fori_loop(0, last, serve, 0)
+    near = order_place(last)
+    request_copy(2 * depth - near).wait_recv()
+    chosen[near, first_span] = select(near, first_rows)
+    for piece in parts[0]:
+        value_copy(near, piece, len(parts)).start()
 
     pl.when(between & jnp.logical_not(upper))(hand_down)
 
@@ -265,6 +263,11 @@
         for step in range(last):
             for piece in parts[later]:
                 value_copy(order_place(step), piece, later).start()
+    chosen[near, other_span] = select(near, other_rows)
+    for part in parts[1:]:
+        for piece in part:
+            value_copy(near, piece, len(parts) + 1).start()
+
     pltpu.make_async_copy(weights, weights, weight_sem).wait()
 
     def slot_of(place):
@@ -273,12 +276,18 @@
             slot = jnp.where(place == k, slots[k], slot)
         return slot
 
-    tally(arrived.at[0, pl.ds(0, sent_rows)], val_send, val_recv.at[len(parts)]).wait_recv()
-    beside = [(arrived[depth], slots[depth]), (arrived[near], slot_of(near))]
+    values = arrived[depth]
     for part in range(levs):
-        total[part] = sum(
-            jnp.dot(value, weights[slot, part], preferred_element_type=jnp.float32) for value, slot in beside
-        )
+        total[part] = jnp.dot(values, weights[slots[depth], part], preferred_element_type=jnp.float32)
+    near_slot = slot_of(near)
+
+    def add_near(span, arrivals, sign):
+        tally(arrived.at[0, pl.ds(0, arrivals)], val_send, val_recv.at[sign]).wait_recv()
+        near_values = arrived[near, span]
+        for part in range(levs):
+            total[part, span] += jnp.dot(near_values, weights[near_slot, part], preferred_element_type=jnp.float32)
+
+    add_near(first_span, weight_of[0], len(parts))
 
     def send_others(number):
         for turn in range(1, levs - 1):
@@ -326,6 +335,8 @@
                 send_others(member)
             else:
                 pl.when(jnp.logical_not(upper))(functools.partial(send_others, member))
+        if number == 0:
+            add_near(other_span, sent_rows - weight_of[0], len(parts) + 1)
 
     bracket_copy.wait()
     fraction_copy.wait()
@@ -459,7 +470,7 @@
             dma,
             dma((count,)),
             dma,
-            dma((len(plan) + 1,)),
+            dma((len(plan) + 2,)),
             dma,
             dma((len(plan) + 1,)),
             pltpu.SemaphoreType.REGULAR,

time: 22.7 us -> 22.5 us (level)
  the two profiles are of different devices: /device:TPU:11 before, /device:TPU:0 now
where the time goes in v5:
time: 22.5 us; the launch traced here: 22.1 us
  Pallas kernels  22.1 us (98%)
    pallas_call x1, Pallas kernels, local(): pl.pallas_call(functools.partial(regrid_kernel, groups, levs, depth), nam...  21.3 us
    pallas_call x1, Pallas kernels, local(): pl.pallas_call(store_kernel, name='store', out_shape=jax.ShapeDtypeStruct...  0.85 us

profile of v5, /device:TPU:0, one launch (start us, length us, event | category | flops | bytes accessed | tf_op | source)
XLA Modules:
  0.0 22.1 jit_solution(938248368093885035)
XLA Ops:
  0.0 21.3 %regrid.1.held_ref = bf16[5,127,512]{2,1,0:T(8,128)(2,1)S(1)} custom-call(s32[5]{0:T(128)} %inter_hbm.1, s32[5,512]{1,0:T(8,128)} %index_hbm.1, bf16[5,17,4096]{2,1,0:T(8,128)(2,1)} %source_hbm.1, bf16[5,512,2048]{2,1,0:T(8,128)(2,1)} %blocks_hbm.1, s32[127,512]{1,0:T(8,128)} %bracket_hbm.1, f32[127,512]{1,0:T(8,128)} %fraction_hbm.1), custom_call_target="tpu_custom_call" | custom-call | flops 3019898880 | bytes 11182080 | tf_op jit(solution)/shard_map/regrid/pallas_call | solution.py:439
  21.3 0.8 %store.1 = bf16[5,127,512]{2,1,0:T(8,128)(2,1)} custom-call(bf16[5,127,512]{2,1,0:T(8,128)(2,1)S(1)} %regrid.1.held_ref), custom_call_target="tpu_custom_call" | custom-call | tf_op jit(solution)/shard_map/store/pallas_call | solution.py:487

commit v6 on v4

--- a/solution.py
+++ b/solution.py
@@ -26,8 +26,7 @@
 
 def field_groups(fields):
     first = max(1, fields // 5)
-    second = (fields - first + 1) // 2
-    cuts = [0, first, first + second, (first + second + fields) // 2, fields]
+    cuts = [0, first, 2 * first, fields - first, fields]
     return [(a, b) for a, b in zip(cuts[:-1], cuts[1:]) if b > a]
 
 

time: 22.7 us -> 22.5 us (level)
  the two profiles are of different devices: /device:TPU:11 before, /device:TPU:0 now
where the time goes in v6:
time: 22.5 us; the launch traced here: 22.3 us
  Pallas kernels  22.2 us (99%)
    pallas_call x1, Pallas kernels, local(): pl.pallas_call(functools.partial(regrid_kernel, groups, levs, depth), nam...  21.4 us
    pallas_call x1, Pallas kernels, local(): pl.pallas_call(store_kernel, name='store', out_shape=jax.ShapeDtypeStruct...  0.85 us

profile of v6, /device:TPU:0, one launch (start us, length us, event | category | flops | bytes accessed | tf_op | source)
XLA Modules:
  0.0 22.3 jit_solution(8158717964667901717)
XLA Ops:
  0.0 21.4 %regrid.1.held_ref = bf16[5,127,512]{2,1,0:T(8,128)(2,1)S(1)} custom-call(s32[5]{0:T(128)} %inter_hbm.1, s32[5,512]{1,0:T(8,128)} %index_hbm.1, bf16[5,17,4096]{2,1,0:T(8,128)(2,1)} %source_hbm.1, bf16[5,512,2048]{2,1,0:T(8,128)(2,1)} %blocks_hbm.1, s32[127,512]{1,0:T(8,128)} %bracket_hbm.1, f32[127,512]{1,0:T(8,128)} %fraction_hbm.1), custom_call_target="tpu_custom_call" | custom-call | flops 3019898880 | bytes 11182080 | tf_op jit(solution)/shard_map/regrid/pallas_call | solution.py:427
  21.4 0.8 %store.1 = bf16[5,127,512]{2,1,0:T(8,128)(2,1)} custom-call(bf16[5,127,512]{2,1,0:T(8,128)(2,1)S(1)} %regrid.1.held_ref), custom_call_target="tpu_custom_call" | custom-call | tf_op jit(solution)/shard_map/store/pallas_call | solution.py:475
